TPU v7x, 128 devices: a whole 4x4x4 slice. The times are simulated.
128 devices in a mesh: tm: 2 (over z_hi), member: 4 (over y), state: 16 (over z_lo, x, core).
Axes of the slice: x: 4, y: 4, z: 4 (z_hi: 2, z_lo: 2; z = z_hi * 2 + z_lo), core: 2. Of those that a mesh axis runs over, the one named last changes fastest.
Arguments:
- members: bfloat16 [4, 8, 16, 768, 1536], P('tm', 'member', None, 'state'), may hold values from -6 to 6
- slot_grad: float32 [4, 16, 768, 1536], P('tm', None, 'state'), may hold values from -6 to 6
- diffusivity: float32 [768, 1536], P('state'), may hold values from 0.03 to 0.24
- vertical: float32 [16, 16], replicated, may hold values from -0.3 to 2.1, as said below
Outputs:
- control_gradient: float32 [16, 8, 768, 1536], P('tm', 'member', 'state')
Inputs may be any that keep to these rules, and one draw needn't show every extreme that they name: `vertical`: the diagonal entries lie between 0.5 and 2.1.
All inputs are finite; a program needn't handle non-finite values.
Results may differ from a plain program's by a relative error of at most 0.0003.
Values sent between devices are 32-bit elements; how exact they have to be, the bound alone decides.
A program may use at most 128 MiB of HBM per device.

v0:
```python
import functools

import jax
import jax.numpy as jnp
from jax import lax
from jax.experimental import pallas as pl
from jax.experimental.pallas import tpu as pltpu
from jax.sharding import PartitionSpec as P

NSTEP = 4
MESH = pl.DeviceIdType.MESH
LANES = 128


def kernel(
    members, slot_grad, diffusivity, vertical, out,
    mv, gv, cs, co, zr, rb, ps, rsr, sg, kp, hst, hsb, hrt, hrb, w, v,
    ld_sem, kp_sem, z_s, z_r, ref_s, ref_r, rs_s, rs_r, ag_s, ag_r, h_s, h_r,
    *, n_state, scale, n_members,
):
    f32 = jnp.float32
    tm, mb, st = lax.axis_index("tm"), lax.axis_index("member"), lax.axis_index("state")
    levels = mv.shape[3]
    half = levels // 2
    quarter = mv.shape[-1]
    tiles = quarter // LANES
    zpeer = (1 - tm, mb, st)
    up, down = (tm, mb, st - 1), (tm, mb, st + 1)
    has_up, has_down = st > 0, st < n_state - 1

    def turn(i):
        return lax.rem(mb + i, 4)

    def ypeer(i):
        return (tm, turn(i), st)

    def remote(src, dst, send, recv, peer):
        return pltpu.make_async_remote_copy(
            src_ref=src, dst_ref=dst, send_sem=send, recv_sem=recv, device_id=peer, device_id_type=MESH
        )

    def block(j):
        rows = lax.rem(2 * (j // 4), 3) * 16
        q = turn(lax.rem(j, 4))
        return pl.multiple_of(rows, 16), q

    def loads(j):
        r0, q = block(j)
        c0 = pl.multiple_of(q * quarter, LANES)
        return (
            pltpu.make_async_copy(
                members.at[:, :, :, pl.ds(r0, 16), pl.ds(c0, quarter)], mv.at[j], ld_sem.at[j, 0]
            ),
            pltpu.make_async_copy(
                slot_grad.at[:, :, pl.ds(r0, 16), pl.ds(c0, quarter)], gv.at[j], ld_sem.at[j, 1]
            ),
        )

    def start_loads(j, c):
        for copy in loads(j):
            copy.start()
        return c

    lax.fori_loop(0, 12, start_loads, 0)
    kload = pltpu.make_async_copy(diffusivity, kp.at[pl.ds(8, 48)], kp_sem)
    kload.start()

    barrier = pltpu.get_barrier_semaphore()
    pl.semaphore_signal(barrier, inc=1, device_id=zpeer, device_id_type=MESH)
    for i in (1, 2, 3):
        pl.semaphore_signal(barrier, inc=1, device_id=ypeer(i), device_id_type=MESH)

    @pl.when(has_up)
    def _():
        pl.semaphore_signal(barrier, inc=1, device_id=up, device_id_type=MESH)

    @pl.when(has_down)
    def _():
        pl.semaphore_signal(barrier, inc=1, device_id=down, device_id_type=MESH)

    zr[mb, :, 1] = jnp.zeros(zr.shape[1:2] + zr.shape[3:], f32)
    w[pl.ds(0, 8)] = jnp.zeros((8, w.shape[1]), f32)
    w[pl.ds(56, 8)] = jnp.zeros((8, w.shape[1]), f32)

    def z_edge(j, count):
        r0, q = block(j)
        rows, ks = pl.ds(r0, 16), pl.ds(0, count)
        return remote(cs.at[q, :, ks, rows], zr.at[q, :, ks, rows], z_s.at[j], z_r.at[j], zpeer)

    def z_mid(l, i):
        q, rows, n = turn(i), pl.ds(16, 16), 8 + 4 * l + i
        ks = pl.ds(0, 1) if i == 0 else pl.ds(0, 2)
        return remote(cs.at[q, l, ks, rows], zr.at[q, l, ks, rows], z_s.at[n], z_r.at[n], zpeer)

    def ref_copy(s, i):
        r0 = pl.multiple_of(lax.rem(2 * s, 3) * 16, 16)
        src = cs.at[mb, :, 1, pl.ds(r0, 16)]
        return remote(src, rb.at[mb, :, pl.ds(r0, 16)], ref_s.at[s, i - 1], ref_r.at[s, i - 1], ypeer(4 - i))

    def span(u):
        if isinstance(u, int) and u < 2:
            return pl.ds(0, half), pl.ds(32 * u, 16)
        return pl.ds(u - 2, 1), pl.ds(16, 16)

    def rs_copy(u, i):
        lv, rows = span(u)
        q = turn(i)
        return remote(ps.at[q, lv, rows], rsr.at[i - 1, lv, rows], rs_s.at[u, i - 1], rs_r.at[u, i - 1], ypeer(i))

    def ag_copy(u, i):
        lv, rows = span(u)
        here = sg.at[mb, lv, rows]
        return remote(here, here, ag_s.at[u, i - 1], ag_r.at[u, i - 1], ypeer(i))

    def k_up():
        return remote(kp.at[pl.ds(8, 8)], kp.at[pl.ds(56, 8)], h_s.at[0], h_r.at[0], up)

    def k_down():
        return remote(kp.at[pl.ds(48, 8)], kp.at[pl.ds(0, 8)], h_s.at[1], h_r.at[1], down)

    def f_up():
        return remote(hst, hrb, h_s.at[2], h_r.at[2], up)

    def f_down():
        return remote(hsb, hrt, h_s.at[3], h_r.at[3], down)

    def products(j):
        r0, q = block(j)
        rows = pl.ds(r0, 16)
        own = half * tm
        other = half - own

        def tile(n, c):
            k = lax.rem(n, 2)
            lanes = pl.ds(pl.multiple_of((n // 2) * LANES, LANES), LANES)
            part = [
                mv[j, 0, k, m, :, lanes].astype(f32) * gv[j, 0, m, :, lanes]
                + mv[j, 1, k, m, :, lanes].astype(f32) * gv[j, 1, m, :, lanes]
                for m in range(levels)
            ]
            for start, dst in ((other, cs), (own, co)):
                for l in range(half):
                    total = vertical[0, start + l] * part[0]
                    for m in range(1, levels):
                        total = total + vertical[m, start + l] * part[m]
                    dst[q, l, k, rows, lanes] = total
            return c

        lax.fori_loop(0, 2 * tiles, tile, 0)

    def step(j, c):
        r0, q = block(j)
        rows = pl.ds(r0, 16)
        s, i = j // 4, lax.rem(j, 4)
        for copy in loads(j):
            copy.wait()
        products(j)

        @pl.when(j == 0)
        def _():
            pl.semaphore_wait(barrier, 4 + has_up.astype(jnp.int32) + has_down.astype(jnp.int32))

        @pl.when(i == 0)
        def _():
            for n in (1, 2, 3):
                ref_copy(s, n).start()

            def sub(l, c):
                cs[q, l, 0, rows] = cs[q, l, 0, rows] - cs[q, l, 1, rows]
                return c

            lax.fori_loop(0, half, sub, 0)

            @pl.when(s < 2)
            def _():
                z_edge(j, 1).start()

        @pl.when(i > 0)
        def _():
            pltpu.make_async_remote_copy(
                src_ref=rb.at[q, :, rows], dst_ref=rb.at[q, :, rows],
                send_sem=ref_s.at[s, i - 1], recv_sem=ref_r.at[s, i - 1],
                device_id=zpeer, device_id_type=MESH,
            ).wait_recv()

            def sub(l, c):
                ref = rb[q, l, rows]
                cs[q, l, 0, rows] = cs[q, l, 0, rows] - ref
                cs[q, l, 1, rows] = cs[q, l, 1, rows] - ref
                return c

            lax.fori_loop(0, half, sub, 0)

            @pl.when(s < 2)
            def _():
                z_edge(j, 2).start()

        return c

    lax.fori_loop(0, 12, step, 0)

    kload.wait()

    @pl.when(has_up)
    def _():
        k_up().start()

    @pl.when(has_down)
    def _():
        k_down().start()

    @pl.when(jnp.logical_not(has_up))
    def _():
        kp[pl.ds(0, 8)] = jnp.zeros((8, kp.shape[1]), f32)
        hrt[...] = jnp.zeros(hrt.shape, f32)

    @pl.when(jnp.logical_not(has_down))
    def _():
        kp[pl.ds(56, 8)] = jnp.zeros((8, kp.shape[1]), f32)
        hrb[...] = jnp.zeros(hrb.shape, f32)

    def add_up(q, l, rows):
        a = co[q, l, 0, rows] + zr[q, l, 0, rows]
        b = co[q, l, 1, rows] + zr[q, l, 1, rows]
        co[q, l, 0, rows] = a
        co[q, l, 1, rows] = b
        ps[q, l, rows] = a + b

    def arrive_edge(u, i):
        z_edge(4 * u + i, 2 if i else 1).wait_recv()
        q = turn(i)

        def body(l, c):
            add_up(q, l, pl.ds(32 * u, 16))
            return c

        lax.fori_loop(0, half, body, 0)
        if i:
            rs_copy(u, i).start()

    def arrive_mid(l):
        for i in range(4):
            z_mid(l, i).wait_recv()
            add_up(turn(i), l, pl.ds(16, 16))
            if i:
                rs_copy(2 + l, i).start()

    def total(u):
        lv, rows = span(u)
        for i in (1, 2, 3):
            rs_copy(u, i).wait_recv()

        def body(l, c):
            sg[mb, l, rows] = (ps[mb, l, rows] + rsr[0, l, rows]) + (rsr[1, l, rows] + rsr[2, l, rows])
            return c

        lax.fori_loop(lv.start, lv.start + lv.size, body, 0)
        for i in (1, 2, 3):
            ag_copy(u, i).start()

    def centred(u):
        lv, rows = span(u)
        for i in (1, 2, 3):
            q = turn(i)
            pltpu.make_async_remote_copy(
                src_ref=sg.at[q, lv, rows], dst_ref=sg.at[q, lv, rows],
                send_sem=ag_s.at[u, 3 - i], recv_sem=ag_r.at[u, 3 - i],
                device_id=zpeer, device_id_type=MESH,
            ).wait_recv()

        def body(l, c):
            for q in range(4):
                mean = sg[q, l, rows] * (1.0 / n_members)
                for k in range(2):
                    out[l, k, rows, pl.ds(q * quarter, quarter)] = (co[q, l, k, rows] - mean) * scale
            return c

        lax.fori_loop(lv.start, lv.start + lv.size, body, 0)

    def edge_top():
        def body(l, c):
            for k in range(2):
                hst[l, pl.ds(4 * k, 4)] = out[l, k, pl.ds(0, 4)]
            return c

        @pl.when(has_up)
        def _():
            lax.fori_loop(0, half, body, 0)
            f_up().start()

    def edge_bottom():
        def body(l, c):
            for k in range(2):
                hsb[l, pl.ds(4 * k, 4)] = out[l, k, pl.ds(44, 4)]
            return c

        @pl.when(has_down)
        def _():
            lax.fori_loop(0, half, body, 0)
            f_down().start()

    def smooth(l):
        for k in range(2):
            w[pl.ds(8, 48)] = out[l, k]
            w[pl.ds(4, 4)] = hrt[l, pl.ds(4 * k, 4)]
            w[pl.ds(56, 4)] = hrb[l, pl.ds(4 * k, 4)]

            def filter_step(n, c):
                for t in range(8):
                    v[pl.ds(8 * t + 8, 8)] = kp[pl.ds(8 * t, 8)] * w[pl.ds(8 * t, 8)]
                for t in range(8):
                    mid = v[pl.ds(8 * t + 8, 8)]
                    around = v[pl.ds(8 * t + 9, 8)] + v[pl.ds(8 * t + 7, 8)]
                    around = around + (pltpu.roll(mid, 1, 1) + pltpu.roll(mid, mid.shape[1] - 1, 1))
                    w[pl.ds(8 * t, 8)] = (w[pl.ds(8 * t, 8)] - 4.0 * mid) + around
                return c

            lax.fori_loop(0, NSTEP, filter_step, 0)
            out[l, k] = w[pl.ds(8, 48)]

    def wait_halos():
        @pl.when(has_up)
        def _():
            k_down().wait_recv()
            f_down().wait_recv()

        @pl.when(has_down)
        def _():
            k_up().wait_recv()
            f_up().wait_recv()

    v[pl.ds(0, 8)] = jnp.zeros((8, v.shape[1]), f32)
    v[pl.ds(72, 8)] = jnp.zeros((8, v.shape[1]), f32)

    def start_mid(l):
        for i in range(4):
            z_mid(l, i).start()

    for i in range(4):
        start_mid(i)
        arrive_edge(0, i)
    start_mid(4)
    arrive_edge(1, 0)
    total(0)
    start_mid(5)
    arrive_edge(1, 1)
    centred(0)
    edge_top()
    start_mid(6)
    arrive_edge(1, 2)
    start_mid(7)
    arrive_edge(1, 3)
    arrive_mid(0)
    total(1)
    arrive_mid(1)
    centred(1)
    edge_bottom()
    total(2)
    wait_halos()

    def rest(l, c):
        arrive_mid(l)
        total(l + 1)
        centred(l)
        smooth(l - 2)
        return c

    lax.fori_loop(2, half, rest, 0)
    total(half + 1)
    centred(half)
    smooth(half - 2)
    centred(half + 1)
    smooth(half - 1)

    for j in range(8):
        z_edge(j, 2 if j % 4 else 1).wait_send()

    def sent(l, c):
        for i in range(4):
            z_mid(l, i).wait_send()
        return c

    lax.fori_loop(0, half, sent, 0)
    for i in (1, 2, 3):
        for s in range(3):
            ref_copy(s, i).wait_send()
        for u in (0, 1):
            rs_copy(u, i).wait_send()
            ag_copy(u, i).wait_send()

    def sums_sent(u, c):
        for i in (1, 2, 3):
            rs_copy(u, i).wait_send()
            ag_copy(u, i).wait_send()
        return c

    lax.fori_loop(2, half + 2, sums_sent, 0)

    @pl.when(has_up)
    def _():
        k_up().wait_send()
        f_up().wait_send()

    @pl.when(has_down)
    def _():
        k_down().wait_send()
        f_down().wait_send()


def body(members, slot_grad, diffusivity, vertical, *, sizes):
    slots, pair, levels, rows, lon = members.shape
    half, quarter = levels // sizes["tm"], lon // 4
    n_members = pair * sizes["member"]
    dma = pltpu.SemaphoreType.DMA
    f32 = jnp.float32
    field = (4, half, pair, rows, quarter)
    one = (4, half, rows, quarter)
    scratch = [
        pltpu.VMEM((12, slots, pair, levels, 16, quarter), members.dtype),
        pltpu.VMEM((12, slots, levels, 16, quarter), f32),
        pltpu.VMEM(field, f32),
        pltpu.VMEM(field, f32),
        pltpu.VMEM(field, f32),
        pltpu.VMEM(one, f32),
        pltpu.VMEM(one, f32),
        pltpu.VMEM((3,) + one[1:], f32),
        pltpu.VMEM(one, f32),
        pltpu.VMEM((64, lon), f32),
        pltpu.VMEM((half, 8, lon), f32),
        pltpu.VMEM((half, 8, lon), f32),
        pltpu.VMEM((half, 8, lon), f32),
        pltpu.VMEM((half, 8, lon), f32),
        pltpu.VMEM((64, lon), f32),
        pltpu.VMEM((80, lon), f32),
        dma((12, 2)),
        dma,
        dma((8 + 4 * half,)),
        dma((8 + 4 * half,)),
        dma((3, 3)),
        dma((3, 3)),
        dma((half + 2, 3)),
        dma((half + 2, 3)),
        dma((half + 2, 3)),
        dma((half + 2, 3)),
        dma((4,)),
        dma((4,)),
    ]
    hbm = pl.BlockSpec(memory_space=pl.ANY)
    return pl.pallas_call(
        functools.partial(
            kernel, n_state=sizes["state"], scale=float(n_members - 1) ** -0.5, n_members=n_members
        ),
        out_shape=jax.ShapeDtypeStruct((half, pair, rows, lon), f32),
        in_specs=[hbm, hbm, hbm, pl.BlockSpec(memory_space=pltpu.SMEM)],
        out_specs=pl.BlockSpec(memory_space=pltpu.VMEM),
        scratch_shapes=scratch,
        compiler_params=pltpu.CompilerParams(
            collective_id=0, has_side_effects=True, vmem_limit_bytes=VMEM_LIMIT
        ),
    )(members, slot_grad, diffusivity, vertical)


VMEM_LIMIT = 56 * 1024 * 1024


def solution(mesh):
    in_specs = (
        P("tm", "member", None, "state", None),
        P("tm", None, "state", None),
        P("state", None),
        P(),
    )
    out_specs = P("tm", "member", "state", None)
    step = functools.partial(body, sizes=dict(mesh.shape))
    return jax.shard_map(step, mesh=mesh, in_specs=in_specs, out_specs=out_specs, check_vma=False)
```

profile of v0, /device:TPU:38, one launch (start us, length us, event | category | flops | bytes accessed | tf_op | source)
XLA Modules:
  0.0 134.0 jit_solution(1793661907670938588)
XLA Ops:
  0.0 129.0 %shard_map.46 = f32[8,2,48,1536]{3,2,1,0:T(8,128)} custom-call(bf16[2,2,16,48,1536]{4,3,2,1,0:T(8,128)(2,1)} %members.1, f32[2,16,48,1536]{3,2,1,0:T(8,128)} %slot_grad.1, f32[48,1536]{1,0:T(8,128)} %diffusivity.1, f32[16,16]{1,0:T(8,128)} %vertical.1), custom_call_target="tpu_custom_call" | custom-call | tf_op jit(solution)/shard_map/pallas_call | solution.py:449
  129.0 5.0 %copy.6 = f32[8,2,48,1536]{3,2,1,0:T(8,128)} copy(f32[8,2,48,1536]{3,2,1,0:T(8,128)} %shard_map.46) | data formatting | bytes 9437184
where the time goes:
time: 134 us
  Pallas kernels  129 us (96%)
  local copies, waits for them, and re-layouts  4.96 us (4%)
    pallas_call x1, Pallas kernels, body(): pl.pallas_call(functools.partial(kernel, n_state=sizes['state'], scale=fl...  129 us
    unnamed x1, local copies, waits for them, and re-layouts  4.96 us

commit v1 on v0

--- a/solution.py
+++ b/solution.py
@@ -13,15 +13,17 @@
 
 
 def kernel(
-    members, slot_grad, diffusivity, vertical, out,
-    mv, gv, cs, co, zr, rb, ps, rsr, sg, kp, hst, hsb, hrt, hrb, w, v,
-    ld_sem, kp_sem, z_s, z_r, ref_s, ref_r, rs_s, rs_r, ag_s, ag_r, h_s, h_r,
+    members, slot_grad, diffusivity, matrix, out,
+    vertical, pp, pr, pg, mv, gv, cs, co, zr, rb, ps, rsr, sg, kp, hst, hsb, hrt, hrb, w, v,
+    v_sem, pre_rs_s, pre_rs_r, pre_ag_s, pre_ag_r, ld_sem, kp_sem, z_s, z_r, ref_s, ref_r, rs_s, rs_r, ag_s, ag_r, h_s, h_r,
     *, n_state, scale, n_members,
 ):
     f32 = jnp.float32
     tm, mb, st = lax.axis_index("tm"), lax.axis_index("member"), lax.axis_index("state")
     levels = mv.shape[3]
     half = levels // 2
+    last = half - 1
+    mid = pl.ds(8, 32)
     quarter = mv.shape[-1]
     tiles = quarter // LANES
     zpeer = (1 - tm, mb, st)
@@ -39,31 +41,25 @@
             src_ref=src, dst_ref=dst, send_sem=send, recv_sem=recv, device_id=peer, device_id_type=MESH
         )
 
-    def block(j):
-        rows = lax.rem(2 * (j // 4), 3) * 16
-        q = turn(lax.rem(j, 4))
-        return pl.multiple_of(rows, 16), q
-
-    def loads(j):
-        r0, q = block(j)
-        c0 = pl.multiple_of(q * quarter, LANES)
+    block_rows = (0, 32, 16)
+
+    def loads(s, i):
+        rows = pl.ds(block_rows[s], 16)
+        lanes = pl.ds(pl.multiple_of(turn(i) * quarter, LANES), quarter)
+        j = 4 * s + i
         return (
-            pltpu.make_async_copy(
-                members.at[:, :, :, pl.ds(r0, 16), pl.ds(c0, quarter)], mv.at[j], ld_sem.at[j, 0]
-            ),
-            pltpu.make_async_copy(
-                slot_grad.at[:, :, pl.ds(r0, 16), pl.ds(c0, quarter)], gv.at[j], ld_sem.at[j, 1]
-            ),
+            pltpu.make_async_copy(members.at[:, :, :, rows, lanes], mv.at[j], ld_sem.at[j, 0]),
+            pltpu.make_async_copy(slot_grad.at[:, :, rows, lanes], gv.at[j], ld_sem.at[j, 1]),
         )
 
-    def start_loads(j, c):
-        for copy in loads(j):
+    def start_loads(s, i):
+        for copy in loads(s, i):
             copy.start()
-        return c
-
-    lax.fori_loop(0, 12, start_loads, 0)
-    kload = pltpu.make_async_copy(diffusivity, kp.at[pl.ds(8, 48)], kp_sem)
-    kload.start()
+
+    vload = pltpu.make_async_copy(matrix, vertical, v_sem)
+    vload.start()
+    start_loads(0, 0)
+    start_loads(0, 1)
 
     barrier = pltpu.get_barrier_semaphore()
     pl.semaphore_signal(barrier, inc=1, device_id=zpeer, device_id_type=MESH)
@@ -78,29 +74,42 @@
     def _():
         pl.semaphore_signal(barrier, inc=1, device_id=down, device_id_type=MESH)
 
-    zr[mb, :, 1] = jnp.zeros(zr.shape[1:2] + zr.shape[3:], f32)
-    w[pl.ds(0, 8)] = jnp.zeros((8, w.shape[1]), f32)
-    w[pl.ds(56, 8)] = jnp.zeros((8, w.shape[1]), f32)
-
-    def z_edge(j, count):
-        r0, q = block(j)
-        rows, ks = pl.ds(r0, 16), pl.ds(0, count)
-        return remote(cs.at[q, :, ks, rows], zr.at[q, :, ks, rows], z_s.at[j], z_r.at[j], zpeer)
+    kload = pltpu.make_async_copy(diffusivity, kp.at[pl.ds(8, 48)], kp_sem)
+    kload.start()
+    start_loads(0, 2)
+
+    def z_edge(u, i):
+        q, rows = turn(i), pl.ds(40 * u, 8)
+        ks = pl.ds(0, 1 if u == 1 and isinstance(i, int) and i == 0 else 2)
+        n = 4 * u + i
+        return remote(cs.at[q, :, ks, rows], zr.at[q, :, ks, rows], z_s.at[n], z_r.at[n], zpeer)
 
     def z_mid(l, i):
-        q, rows, n = turn(i), pl.ds(16, 16), 8 + 4 * l + i
+        q, n = turn(i), 8 + 4 * l + i
         ks = pl.ds(0, 1) if i == 0 else pl.ds(0, 2)
-        return remote(cs.at[q, l, ks, rows], zr.at[q, l, ks, rows], z_s.at[n], z_r.at[n], zpeer)
+        return remote(cs.at[q, l, ks, mid], zr.at[q, l, ks, mid], z_s.at[n], z_r.at[n], zpeer)
+
+    def z_last(k):
+        n = 8 + 4 * last + k
+        return remote(cs.at[:, last, k, mid], zr.at[:, last, k, mid], z_s.at[n], z_r.at[n], zpeer)
+
+    ref_part = ((pl.ds(0, last), pl.ds(8, 8)), (pl.ds(0, half), pl.ds(32, 16)), (pl.ds(0, last), pl.ds(16, 16)))
 
     def ref_copy(s, i):
-        r0 = pl.multiple_of(lax.rem(2 * s, 3) * 16, 16)
-        src = cs.at[mb, :, 1, pl.ds(r0, 16)]
-        return remote(src, rb.at[mb, :, pl.ds(r0, 16)], ref_s.at[s, i - 1], ref_r.at[s, i - 1], ypeer(4 - i))
+        lv, rows = ref_part[s]
+        return remote(
+            cs.at[mb, lv, 1, rows], rb.at[mb, lv, rows], ref_s.at[s, i - 1], ref_r.at[s, i - 1], ypeer(4 - i)
+        )
+
+    def ref_arrival(s, i):
+        lv, rows = ref_part[s]
+        here = rb.at[turn(i), lv, rows]
+        return remote(here, here, ref_s.at[s, i - 1], ref_r.at[s, i - 1], zpeer)
 
     def span(u):
         if isinstance(u, int) and u < 2:
-            return pl.ds(0, half), pl.ds(32 * u, 16)
-        return pl.ds(u - 2, 1), pl.ds(16, 16)
+            return pl.ds(0, half), pl.ds(40 * u, 8)
+        return pl.ds(u - 2, 1), mid
 
     def rs_copy(u, i):
         lv, rows = span(u)
@@ -112,6 +121,12 @@
         here = sg.at[mb, lv, rows]
         return remote(here, here, ag_s.at[u, i - 1], ag_r.at[u, i - 1], ypeer(i))
 
+    def pre_rs(i):
+        return remote(pp.at[turn(i)], pr.at[i - 1], pre_rs_s.at[i - 1], pre_rs_r.at[i - 1], ypeer(i))
+
+    def pre_ag(i):
+        return remote(pg.at[mb], pg.at[mb], pre_ag_s.at[i - 1], pre_ag_r.at[i - 1], ypeer(i))
+
     def k_up():
         return remote(kp.at[pl.ds(8, 8)], kp.at[pl.ds(56, 8)], h_s.at[0], h_r.at[0], up)
 
@@ -124,9 +139,9 @@
     def f_down():
         return remote(hsb, hrt, h_s.at[3], h_r.at[3], down)
 
-    def products(j):
-        r0, q = block(j)
-        rows = pl.ds(r0, 16)
+    def products(s, i):
+        j, q = 4 * s + i, turn(i)
+        rows = pl.ds(block_rows[s], 16)
         own = half * tm
         other = half - own
 
@@ -148,56 +163,70 @@
 
         lax.fori_loop(0, 2 * tiles, tile, 0)
 
-    def step(j, c):
-        r0, q = block(j)
-        rows = pl.ds(r0, 16)
-        s, i = j // 4, lax.rem(j, 4)
-        for copy in loads(j):
-            copy.wait()
-        products(j)
-
-        @pl.when(j == 0)
-        def _():
-            pl.semaphore_wait(barrier, 4 + has_up.astype(jnp.int32) + has_down.astype(jnp.int32))
-
-        @pl.when(i == 0)
-        def _():
-            for n in (1, 2, 3):
-                ref_copy(s, n).start()
+    ref_tiles = (((8, last),), ((32, last), (40, half)), ((16, last), (24, last)))
+
+    def subtract(s, q, refer, ks):
+        for r, count in ref_tiles[s]:
+            rows = pl.ds(r, 8)
 
             def sub(l, c):
-                cs[q, l, 0, rows] = cs[q, l, 0, rows] - cs[q, l, 1, rows]
+                ref = refer(l, rows)
+                for k in ks:
+                    cs[q, l, k, rows] = cs[q, l, k, rows] - ref
                 return c
 
-            lax.fori_loop(0, half, sub, 0)
-
-            @pl.when(s < 2)
+            lax.fori_loop(0, count, sub, 0)
+
+    def mix(s):
+        def step(i, c):
+            for ahead in range(4):
+                at, to = (s, ahead + 3) if ahead == 0 else (s + 1, ahead - 1)
+                if at < 3:
+
+                    @pl.when(i == ahead)
+                    def _():
+                        start_loads(at, to)
+
+            for copy in loads(s, i):
+                copy.wait()
+            products(s, i)
+            if s == 0:
+
+                @pl.when(i == 0)
+                def _():
+                    peers = 4 + has_up.astype(jnp.int32) + has_down.astype(jnp.int32)
+                    pl.semaphore_wait(barrier, peers)
+
+                z_edge(0, i).start()
+
+            @pl.when(i == 0)
             def _():
-                z_edge(j, 1).start()
-
-        @pl.when(i > 0)
-        def _():
-            pltpu.make_async_remote_copy(
-                src_ref=rb.at[q, :, rows], dst_ref=rb.at[q, :, rows],
-                send_sem=ref_s.at[s, i - 1], recv_sem=ref_r.at[s, i - 1],
-                device_id=zpeer, device_id_type=MESH,
-            ).wait_recv()
-
-            def sub(l, c):
-                ref = rb[q, l, rows]
-                cs[q, l, 0, rows] = cs[q, l, 0, rows] - ref
-                cs[q, l, 1, rows] = cs[q, l, 1, rows] - ref
-                return c
-
-            lax.fori_loop(0, half, sub, 0)
-
-            @pl.when(s < 2)
-            def _():
-                z_edge(j, 2).start()
-
-        return c
-
-    lax.fori_loop(0, 12, step, 0)
+                for n in (1, 2, 3):
+                    ref_copy(s, n).start()
+                subtract(s, mb, lambda l, rows: cs[mb, l, 1, rows], (0,))
+                if s == 1:
+                    z_edge(1, 0).start()
+
+            return c
+
+        lax.fori_loop(0, 4, step, 0)
+
+    def refer(s):
+        def step(i, c):
+            q = turn(i)
+            ref_arrival(s, i).wait_recv()
+            subtract(s, q, lambda l, rows: rb[q, l, rows], (0, 1))
+            if s == 1:
+                z_edge(1, i).start()
+            return c
+
+        lax.fori_loop(1, 4, step, 0)
+
+    vload.wait()
+    for s in range(3):
+        mix(s)
+    for s in (1, 0, 2):
+        refer(s)
 
     kload.wait()
 
@@ -227,11 +256,11 @@
         ps[q, l, rows] = a + b
 
     def arrive_edge(u, i):
-        z_edge(4 * u + i, 2 if i else 1).wait_recv()
+        z_edge(u, i).wait_recv()
         q = turn(i)
 
         def body(l, c):
-            add_up(q, l, pl.ds(32 * u, 16))
+            add_up(q, l, pl.ds(40 * u, 8))
             return c
 
         lax.fori_loop(0, half, body, 0)
@@ -241,7 +270,7 @@
     def arrive_mid(l):
         for i in range(4):
             z_mid(l, i).wait_recv()
-            add_up(turn(i), l, pl.ds(16, 16))
+            add_up(turn(i), l, mid)
             if i:
                 rs_copy(2 + l, i).start()
 
@@ -277,6 +306,38 @@
 
         lax.fori_loop(lv.start, lv.start + lv.size, body, 0)
 
+    def pre_sum():
+        for n in range(4):
+            q = turn(n)
+            for h, src in enumerate((cs, co)):
+                pp[q, h] = src[q, last, 0, mid] + src[q, last, 1, mid]
+            if n:
+                pre_rs(n).start()
+
+    def pre_total():
+        for i in (1, 2, 3):
+            pre_rs(i).wait_recv()
+        for h in range(2):
+            pg[mb, h] = (pp[mb, h] + pr[0, h]) + (pr[1, h] + pr[2, h])
+        for i in (1, 2, 3):
+            pre_ag(i).start()
+
+    def pre_centred():
+        for i in (1, 2, 3):
+            here = pg.at[turn(i)]
+            remote(here, here, pre_ag_s.at[3 - i], pre_ag_r.at[3 - i], zpeer).wait_recv()
+            ref_copy(1, i).wait_send()
+        for q in range(4):
+            for h, dst in enumerate((cs, co)):
+                mean = pg[q, h] * (1.0 / n_members)
+                for k in range(2):
+                    dst[q, last, k, mid] = dst[q, last, k, mid] - mean
+
+    def arrive_last(k):
+        z_last(k).wait_recv()
+        for q in range(4):
+            out[last, k, mid, pl.ds(q * quarter, quarter)] = (co[q, last, k, mid] + zr[q, last, k, mid]) * scale
+
     def edge_top():
         def body(l, c):
             for k in range(2):
@@ -299,8 +360,8 @@
             lax.fori_loop(0, half, body, 0)
             f_down().start()
 
-    def smooth(l):
-        for k in range(2):
+    def smooth(l, ks=(0, 1)):
+        for k in ks:
             w[pl.ds(8, 48)] = out[l, k]
             w[pl.ds(4, 4)] = hrt[l, pl.ds(4 * k, 4)]
             w[pl.ds(56, 4)] = hrb[l, pl.ds(4 * k, 4)]
@@ -329,6 +390,10 @@
             k_up().wait_recv()
             f_up().wait_recv()
 
+    w[pl.ds(0, 8)] = jnp.zeros((8, w.shape[1]), f32)
+    w[pl.ds(56, 8)] = jnp.zeros((8, w.shape[1]), f32)
+    zr[mb, pl.ds(0, last), 1, pl.ds(8, 40)] = jnp.zeros((last, 40, quarter), f32)
+    zr[mb, last, 1, pl.ds(40, 8)] = jnp.zeros((8, quarter), f32)
     v[pl.ds(0, 8)] = jnp.zeros((8, v.shape[1]), f32)
     v[pl.ds(72, 8)] = jnp.zeros((8, v.shape[1]), f32)
 
@@ -336,53 +401,69 @@
         for i in range(4):
             z_mid(l, i).start()
 
+    pre_sum()
+    start_mid(0)
+    start_mid(1)
     for i in range(4):
-        start_mid(i)
         arrive_edge(0, i)
-    start_mid(4)
+    start_mid(2)
+    pre_total()
     arrive_edge(1, 0)
     total(0)
-    start_mid(5)
+    start_mid(3)
     arrive_edge(1, 1)
+    pre_centred()
+    arrive_edge(1, 2)
     centred(0)
     edge_top()
+    start_mid(4)
+    arrive_edge(1, 3)
+    start_mid(5)
+    arrive_mid(0)
     start_mid(6)
-    arrive_edge(1, 2)
-    start_mid(7)
-    arrive_edge(1, 3)
-    arrive_mid(0)
+    z_last(0).start()
+    z_last(1).start()
     total(1)
-    arrive_mid(1)
+    total(2)
     centred(1)
     edge_bottom()
-    total(2)
-    wait_halos()
 
     def rest(l, c):
         arrive_mid(l)
-        total(l + 1)
-        centred(l)
-        smooth(l - 2)
+
+        @pl.when(l == 1)
+        def _():
+            wait_halos()
+
+        centred(l + 1)
+        smooth(l - 1)
+        total(l + 2)
         return c
 
-    lax.fori_loop(2, half, rest, 0)
-    total(half + 1)
-    centred(half)
-    smooth(half - 2)
-    centred(half + 1)
-    smooth(half - 1)
-
-    for j in range(8):
-        z_edge(j, 2 if j % 4 else 1).wait_send()
+    lax.fori_loop(1, last, rest, 0)
+    arrive_last(0)
+    smooth(last, (0,))
+    centred(last + 1)
+    smooth(last - 1)
+    arrive_last(1)
+    smooth(last, (1,))
+
+    for u in range(2):
+        for i in range(4):
+            z_edge(u, i).wait_send()
+    for k in range(2):
+        z_last(k).wait_send()
 
     def sent(l, c):
         for i in range(4):
             z_mid(l, i).wait_send()
         return c
 
-    lax.fori_loop(0, half, sent, 0)
+    lax.fori_loop(0, last, sent, 0)
     for i in (1, 2, 3):
-        for s in range(3):
+        pre_rs(i).wait_send()
+        pre_ag(i).wait_send()
+        for s in (0, 2):
             ref_copy(s, i).wait_send()
         for u in (0, 1):
             rs_copy(u, i).wait_send()
@@ -394,7 +475,7 @@
             ag_copy(u, i).wait_send()
         return c
 
-    lax.fori_loop(2, half + 2, sums_sent, 0)
+    lax.fori_loop(2, last + 2, sums_sent, 0)
 
     @pl.when(has_up)
     def _():
@@ -416,6 +497,10 @@
     field = (4, half, pair, rows, quarter)
     one = (4, half, rows, quarter)
     scratch = [
+        pltpu.SMEM((levels, levels), f32),
+        pltpu.VMEM((4, 2, 32, quarter), f32),
+        pltpu.VMEM((3, 2, 32, quarter), f32),
+        pltpu.VMEM((4, 2, 32, quarter), f32),
         pltpu.VMEM((12, slots, pair, levels, 16, quarter), members.dtype),
         pltpu.VMEM((12, slots, levels, 16, quarter), f32),
         pltpu.VMEM(field, f32),
@@ -432,26 +517,31 @@
         pltpu.VMEM((half, 8, lon), f32),
         pltpu.VMEM((64, lon), f32),
         pltpu.VMEM((80, lon), f32),
+        dma,
+        dma((3,)),
+        dma((3,)),
+        dma((3,)),
+        dma((3,)),
         dma((12, 2)),
         dma,
-        dma((8 + 4 * half,)),
-        dma((8 + 4 * half,)),
+        dma((10 + 4 * (half - 1),)),
+        dma((10 + 4 * (half - 1),)),
         dma((3, 3)),
         dma((3, 3)),
-        dma((half + 2, 3)),
-        dma((half + 2, 3)),
-        dma((half + 2, 3)),
-        dma((half + 2, 3)),
+        dma((half + 1, 3)),
+        dma((half + 1, 3)),
+        dma((half + 1, 3)),
+        dma((half + 1, 3)),
         dma((4,)),
         dma((4,)),
     ]
-    hbm = pl.BlockSpec(memory_space=pl.ANY)
+    hbm = pl.BlockSpec(memory_space=pltpu.HBM)
     return pl.pallas_call(
         functools.partial(
             kernel, n_state=sizes["state"], scale=float(n_members - 1) ** -0.5, n_members=n_members
         ),
-        out_shape=jax.ShapeDtypeStruct((half, pair, rows, lon), f32),
-        in_specs=[hbm, hbm, hbm, pl.BlockSpec(memory_space=pltpu.SMEM)],
+        out_shape=pltpu.VMEM((half, pair, rows, lon), f32),
+        in_specs=[hbm] * 4,
         out_specs=pl.BlockSpec(memory_space=pltpu.VMEM),
         scratch_shapes=scratch,
         compiler_params=pltpu.CompilerParams(
@@ -460,7 +550,7 @@
     )(members, slot_grad, diffusivity, vertical)
 
 
-VMEM_LIMIT = 56 * 1024 * 1024
+VMEM_LIMIT = 50 * 1024 * 1024
 
 
 def solution(mesh):

time: 134 us -> 119 us (0.89); the launches traced: 134 us -> 117 us
  Pallas kernels: 129 us -> 115 us
  local copies, waits for them, and re-layouts: 4.96 us -> 2.19 us
    pallas_call x1, Pallas kernels: 129 us -> 115 us  [body(): pl.pallas_call(functools.partial(kernel, n_state=sizes['state'], scale=fl...]
    unnamed x1, local copies, waits for them, and re-layouts: 4.96 us -> 2.19 us
where the time goes in v1:
time: 119 us; the launch traced here: 117 us
  Pallas kernels  115 us (97%)
  local copies, waits for them, and re-layouts  2.19 us (2%)
    pallas_call x1, Pallas kernels, body(): pl.pallas_call(functools.partial(kernel, n_state=sizes['state'], scale=fl...  115 us

profile of v1, /device:TPU:38, one launch (start us, length us, event | category | flops | bytes accessed | tf_op | source)
XLA Modules:
  0.0 117.2 jit_solution(13298420876544538395)
XLA Ops:
  0.0 115.0 %shard_map.46 = f32[8,2,48,1536]{3,2,1,0:T(8,128)S(1)} custom-call(bf16[2,2,16,48,1536]{4,3,2,1,0:T(8,128)(2,1)} %members.1, f32[2,16,48,1536]{3,2,1,0:T(8,128)} %slot_grad.1, f32[48,1536]{1,0:T(8,128)} %diffusivity.1, f32[16,16]{1,0:T(8,128)} %matrix.1), custom_call_target="tpu_custom_call" | custom-call | tf_op jit(solution)/shard_map/pallas_call | solution.py:539
  115.0 2.2 %copy.6 = f32[8,2,48,1536]{3,2,1,0:T(8,128)} copy(f32[8,2,48,1536]{3,2,1,0:T(8,128)S(1)} %shard_map.46) | data formatting | bytes 9437184

commit v2 on v1

--- a/solution.py
+++ b/solution.py
@@ -22,7 +22,7 @@
     tm, mb, st = lax.axis_index("tm"), lax.axis_index("member"), lax.axis_index("state")
     levels = mv.shape[3]
     half = levels // 2
-    last = half - 1
+    post = half - 2
     mid = pl.ds(8, 32)
     quarter = mv.shape[-1]
     tiles = quarter // LANES
@@ -59,7 +59,7 @@
     vload = pltpu.make_async_copy(matrix, vertical, v_sem)
     vload.start()
     start_loads(0, 0)
-    start_loads(0, 1)
+    start_loads(1, 0)
 
     barrier = pltpu.get_barrier_semaphore()
     pl.semaphore_signal(barrier, inc=1, device_id=zpeer, device_id_type=MESH)
@@ -76,7 +76,7 @@
 
     kload = pltpu.make_async_copy(diffusivity, kp.at[pl.ds(8, 48)], kp_sem)
     kload.start()
-    start_loads(0, 2)
+    start_loads(0, 1)
 
     def z_edge(u, i):
         q, rows = turn(i), pl.ds(40 * u, 8)
@@ -89,11 +89,12 @@
         ks = pl.ds(0, 1) if i == 0 else pl.ds(0, 2)
         return remote(cs.at[q, l, ks, mid], zr.at[q, l, ks, mid], z_s.at[n], z_r.at[n], zpeer)
 
-    def z_last(k):
-        n = 8 + 4 * last + k
-        return remote(cs.at[:, last, k, mid], zr.at[:, last, k, mid], z_s.at[n], z_r.at[n], zpeer)
-
-    ref_part = ((pl.ds(0, last), pl.ds(8, 8)), (pl.ds(0, half), pl.ds(32, 16)), (pl.ds(0, last), pl.ds(16, 16)))
+    def z_last(n):
+        at = 8 + 4 * post + n
+        l, k = post + n // 2, n % 2
+        return remote(cs.at[:, l, k, mid], zr.at[:, l, k, mid], z_s.at[at], z_r.at[at], zpeer)
+
+    ref_part = ((pl.ds(0, post), pl.ds(8, 8)), (pl.ds(0, half), pl.ds(32, 16)), (pl.ds(0, post), pl.ds(16, 16)))
 
     def ref_copy(s, i):
         lv, rows = ref_part[s]
@@ -163,7 +164,7 @@
 
         lax.fori_loop(0, 2 * tiles, tile, 0)
 
-    ref_tiles = (((8, last),), ((32, last), (40, half)), ((16, last), (24, last)))
+    ref_tiles = (((8, post),), ((32, post), (40, half)), ((16, post), (24, post)))
 
     def subtract(s, q, refer, ks):
         for r, count in ref_tiles[s]:
@@ -177,39 +178,29 @@
 
             lax.fori_loop(0, count, sub, 0)
 
-    def mix(s):
+    def mix(s, i):
+        for copy in loads(s, i):
+            copy.wait()
+        products(s, i)
+        if isinstance(i, int) and i == 0:
+            if s == 0:
+                peers = 4 + has_up.astype(jnp.int32) + has_down.astype(jnp.int32)
+                pl.semaphore_wait(barrier, peers)
+            for n in (1, 2, 3):
+                ref_copy(s, n).start()
+            if s == 0:
+                z_edge(0, i).start()
+            subtract(s, mb, lambda l, rows: cs[mb, l, 1, rows], (0,))
+        elif s == 0:
+            z_edge(0, i).start()
+
+    def mix_rest(s, after):
         def step(i, c):
-            for ahead in range(4):
-                at, to = (s, ahead + 3) if ahead == 0 else (s + 1, ahead - 1)
-                if at < 3:
-
-                    @pl.when(i == ahead)
-                    def _():
-                        start_loads(at, to)
-
-            for copy in loads(s, i):
-                copy.wait()
-            products(s, i)
-            if s == 0:
-
-                @pl.when(i == 0)
-                def _():
-                    peers = 4 + has_up.astype(jnp.int32) + has_down.astype(jnp.int32)
-                    pl.semaphore_wait(barrier, peers)
-
-                z_edge(0, i).start()
-
-            @pl.when(i == 0)
-            def _():
-                for n in (1, 2, 3):
-                    ref_copy(s, n).start()
-                subtract(s, mb, lambda l, rows: cs[mb, l, 1, rows], (0,))
-                if s == 1:
-                    z_edge(1, 0).start()
-
-            return c
-
-        lax.fori_loop(0, 4, step, 0)
+            after(i)
+            mix(s, i)
+            return c
+
+        lax.fori_loop(1, 4, step, 0)
 
     def refer(s):
         def step(i, c):
@@ -223,10 +214,19 @@
         lax.fori_loop(1, 4, step, 0)
 
     vload.wait()
-    for s in range(3):
-        mix(s)
-    for s in (1, 0, 2):
-        refer(s)
+    start_loads(0, 2)
+    mix(0, 0)
+    start_loads(0, 3)
+    mix(1, 0)
+    mix_rest(0, lambda i: start_loads(1, i))
+    z_edge(1, 0).start()
+    mix_rest(1, lambda i: start_loads(2, i - 1))
+    refer(1)
+    start_loads(2, 3)
+    mix(2, 0)
+    mix_rest(2, lambda i: None)
+    refer(0)
+    refer(2)
 
     kload.wait()
 
@@ -309,16 +309,26 @@
     def pre_sum():
         for n in range(4):
             q = turn(n)
-            for h, src in enumerate((cs, co)):
-                pp[q, h] = src[q, last, 0, mid] + src[q, last, 1, mid]
+
+            def add(l, c):
+                for h, src in enumerate((cs, co)):
+                    pp[q, h, l] = src[q, post + l, 0, mid] + src[q, post + l, 1, mid]
+                return c
+
+            lax.fori_loop(0, 2, add, 0)
             if n:
                 pre_rs(n).start()
 
     def pre_total():
         for i in (1, 2, 3):
             pre_rs(i).wait_recv()
-        for h in range(2):
-            pg[mb, h] = (pp[mb, h] + pr[0, h]) + (pr[1, h] + pr[2, h])
+
+        def add(l, c):
+            for h in range(2):
+                pg[mb, h, l] = (pp[mb, h, l] + pr[0, h, l]) + (pr[1, h, l] + pr[2, h, l])
+            return c
+
+        lax.fori_loop(0, 2, add, 0)
         for i in (1, 2, 3):
             pre_ag(i).start()
 
@@ -327,16 +337,22 @@
             here = pg.at[turn(i)]
             remote(here, here, pre_ag_s.at[3 - i], pre_ag_r.at[3 - i], zpeer).wait_recv()
             ref_copy(1, i).wait_send()
+
+        def centre(q, c):
+            for l in range(2):
+                for h, dst in enumerate((cs, co)):
+                    mean = pg[q, h, l] * (1.0 / n_members)
+                    for k in range(2):
+                        dst[q, post + l, k, mid] = dst[q, post + l, k, mid] - mean
+            return c
+
+        lax.fori_loop(0, 4, centre, 0)
+
+    def arrive_last(n):
+        z_last(n).wait_recv()
+        l, k = post + n // 2, n % 2
         for q in range(4):
-            for h, dst in enumerate((cs, co)):
-                mean = pg[q, h] * (1.0 / n_members)
-                for k in range(2):
-                    dst[q, last, k, mid] = dst[q, last, k, mid] - mean
-
-    def arrive_last(k):
-        z_last(k).wait_recv()
-        for q in range(4):
-            out[last, k, mid, pl.ds(q * quarter, quarter)] = (co[q, last, k, mid] + zr[q, last, k, mid]) * scale
+            out[l, k, mid, pl.ds(q * quarter, quarter)] = (co[q, l, k, mid] + zr[q, l, k, mid]) * scale
 
     def edge_top():
         def body(l, c):
@@ -366,14 +382,22 @@
             w[pl.ds(4, 4)] = hrt[l, pl.ds(4 * k, 4)]
             w[pl.ds(56, 4)] = hrb[l, pl.ds(4 * k, 4)]
 
+            row = lax.broadcasted_iota(jnp.int32, (8, w.shape[1]), 0)
+            top_row, bottom_row = row == 0, row == 7
+
             def filter_step(n, c):
+                def product(t):
+                    v[pl.ds(8 * t + 8, 8)] = kp[pl.ds(8 * t, 8)] * w[pl.ds(8 * t, 8)]
+
+                product(0)
                 for t in range(8):
-                    v[pl.ds(8 * t + 8, 8)] = kp[pl.ds(8 * t, 8)] * w[pl.ds(8 * t, 8)]
-                for t in range(8):
-                    mid = v[pl.ds(8 * t + 8, 8)]
-                    around = v[pl.ds(8 * t + 9, 8)] + v[pl.ds(8 * t + 7, 8)]
-                    around = around + (pltpu.roll(mid, 1, 1) + pltpu.roll(mid, mid.shape[1] - 1, 1))
-                    w[pl.ds(8 * t, 8)] = (w[pl.ds(8 * t, 8)] - 4.0 * mid) + around
+                    if t < 7:
+                        product(t + 1)
+                    before, at, after = (v[pl.ds(8 * t + 8 * n, 8)] for n in range(3))
+                    around = pltpu.roll(at, 1, 1) + pltpu.roll(at, at.shape[1] - 1, 1)
+                    around = around + pltpu.roll(jnp.where(bottom_row, before, at), 1, 0)
+                    around = around + pltpu.roll(jnp.where(top_row, after, at), 7, 0)
+                    w[pl.ds(8 * t, 8)] = (w[pl.ds(8 * t, 8)] - 4.0 * at) + around
                 return c
 
             lax.fori_loop(0, NSTEP, filter_step, 0)
@@ -392,8 +416,8 @@
 
     w[pl.ds(0, 8)] = jnp.zeros((8, w.shape[1]), f32)
     w[pl.ds(56, 8)] = jnp.zeros((8, w.shape[1]), f32)
-    zr[mb, pl.ds(0, last), 1, pl.ds(8, 40)] = jnp.zeros((last, 40, quarter), f32)
-    zr[mb, last, 1, pl.ds(40, 8)] = jnp.zeros((8, quarter), f32)
+    zr[mb, pl.ds(0, post), 1, pl.ds(8, 40)] = jnp.zeros((post, 40, quarter), f32)
+    zr[mb, pl.ds(post, 2), 1, pl.ds(40, 8)] = jnp.zeros((2, 8, quarter), f32)
     v[pl.ds(0, 8)] = jnp.zeros((8, v.shape[1]), f32)
     v[pl.ds(72, 8)] = jnp.zeros((8, v.shape[1]), f32)
 
@@ -401,65 +425,71 @@
         for i in range(4):
             z_mid(l, i).start()
 
-    pre_sum()
     start_mid(0)
     start_mid(1)
     for i in range(4):
         arrive_edge(0, i)
+    arrive_edge(1, 0)
+    arrive_edge(1, 1)
+    total(0)
     start_mid(2)
-    pre_total()
-    arrive_edge(1, 0)
-    total(0)
+    arrive_edge(1, 2)
+    arrive_edge(1, 3)
     start_mid(3)
-    arrive_edge(1, 1)
-    pre_centred()
-    arrive_edge(1, 2)
+    total(1)
     centred(0)
     edge_top()
+    pre_sum()
     start_mid(4)
-    arrive_edge(1, 3)
     start_mid(5)
     arrive_mid(0)
-    start_mid(6)
-    z_last(0).start()
-    z_last(1).start()
-    total(1)
-    total(2)
     centred(1)
     edge_bottom()
+    arrive_mid(1)
+    total(2)
+    pre_total()
+    arrive_mid(2)
+    total(3)
+    wait_halos()
+    centred(2)
+    smooth(0)
+    pre_centred()
+    for n in range(4):
+        z_last(n).start()
 
     def rest(l, c):
         arrive_mid(l)
-
-        @pl.when(l == 1)
-        def _():
-            wait_halos()
-
-        centred(l + 1)
-        smooth(l - 1)
-        total(l + 2)
+        total(l + 1)
+        centred(l)
+        smooth(l - 2)
         return c
 
-    lax.fori_loop(1, last, rest, 0)
+    lax.fori_loop(3, post, rest, 0)
+    total(post + 1)
+    centred(post)
+    smooth(post - 2)
     arrive_last(0)
-    smooth(last, (0,))
-    centred(last + 1)
-    smooth(last - 1)
+    smooth(post, (0,))
+    centred(post + 1)
+    smooth(post - 1)
     arrive_last(1)
-    smooth(last, (1,))
+    smooth(post, (1,))
+    for k in range(2):
+        arrive_last(2 + k)
+        smooth(post + 1, (k,))
 
     for u in range(2):
         for i in range(4):
             z_edge(u, i).wait_send()
-    for k in range(2):
-        z_last(k).wait_send()
+    for n in range(4):
+        z_last(n).wait_send()
 
     def sent(l, c):
         for i in range(4):
             z_mid(l, i).wait_send()
         return c
 
-    lax.fori_loop(0, last, sent, 0)
+    lax.fori_loop(0, post, sent, 0)
     for i in (1, 2, 3):
         pre_rs(i).wait_send()
         pre_ag(i).wait_send()
@@ -475,7 +505,7 @@
             ag_copy(u, i).wait_send()
         return c
 
-    lax.fori_loop(2, last + 2, sums_sent, 0)
+    lax.fori_loop(2, post + 2, sums_sent, 0)
 
     @pl.when(has_up)
     def _():
@@ -498,9 +528,9 @@
     one = (4, half, rows, quarter)
     scratch = [
         pltpu.SMEM((levels, levels), f32),
-        pltpu.VMEM((4, 2, 32, quarter), f32),
-        pltpu.VMEM((3, 2, 32, quarter), f32),
-        pltpu.VMEM((4, 2, 32, quarter), f32),
+        pltpu.VMEM((4, 2, 2, 32, quarter), f32),
+        pltpu.VMEM((3, 2, 2, 32, quarter), f32),
+        pltpu.VMEM((4, 2, 2, 32, quarter), f32),
         pltpu.VMEM((12, slots, pair, levels, 16, quarter), members.dtype),
         pltpu.VMEM((12, slots, levels, 16, quarter), f32),
         pltpu.VMEM(field, f32),
@@ -524,14 +554,14 @@
         dma((3,)),
         dma((12, 2)),
         dma,
-        dma((10 + 4 * (half - 1),)),
-        dma((10 + 4 * (half - 1),)),
+        dma((12 + 4 * (half - 2),)),
+        dma((12 + 4 * (half - 2),)),
         dma((3, 3)),
         dma((3, 3)),
-        dma((half + 1, 3)),
-        dma((half + 1, 3)),
-        dma((half + 1, 3)),
-        dma((half + 1, 3)),
+        dma((half, 3)),
+        dma((half, 3)),
+        dma((half, 3)),
+        dma((half, 3)),
         dma((4,)),
         dma((4,)),
     ]

time: 119 us -> 111 us (0.933)
  Pallas kernels: 115 us -> 108 us
    pallas_call x1, Pallas kernels: 115 us -> 108 us  [body(): pl.pallas_call(functools.partial(kernel, n_state=sizes['state'], scale=fl...]
where the time goes in v2:
time: 111 us; the launch traced here: 110 us
  Pallas kernels  108 us (97%)
  local copies, waits for them, and re-layouts  2.19 us (2%)
    pallas_call x1, Pallas kernels, body(): pl.pallas_call(functools.partial(kernel, n_state=sizes['state'], scale=fl...  108 us

profile of v2, /device:TPU:38, one launch (start us, length us, event | category | flops | bytes accessed | tf_op | source)
XLA Modules:
  0.0 110.2 jit_solution(210581660134961526)
XLA Ops:
  0.0 108.0 %shard_map.46 = f32[8,2,48,1536]{3,2,1,0:T(8,128)S(1)} custom-call(bf16[2,2,16,48,1536]{4,3,2,1,0:T(8,128)(2,1)} %members.1, f32[2,16,48,1536]{3,2,1,0:T(8,128)} %slot_grad.1, f32[48,1536]{1,0:T(8,128)} %diffusivity.1, f32[16,16]{1,0:T(8,128)} %matrix.1), custom_call_target="tpu_custom_call" | custom-call | tf_op jit(solution)/shard_map/pallas_call | solution.py:569
  108.0 2.2 %copy.6 = f32[8,2,48,1536]{3,2,1,0:T(8,128)} copy(f32[8,2,48,1536]{3,2,1,0:T(8,128)S(1)} %shard_map.46) | data formatting | bytes 9437184

commit v3 on v2

--- a/solution.py
+++ b/solution.py
@@ -14,8 +14,8 @@
 
 def kernel(
     members, slot_grad, diffusivity, matrix, out,
-    vertical, pp, pr, pg, mv, gv, cs, co, zr, rb, ps, rsr, sg, kp, hst, hsb, hrt, hrb, w, v,
-    v_sem, pre_rs_s, pre_rs_r, pre_ag_s, pre_ag_r, ld_sem, kp_sem, z_s, z_r, ref_s, ref_r, rs_s, rs_r, ag_s, ag_r, h_s, h_r,
+    vertical, pp, pr, pg, mv, gv, cs, co, zr, rb, ps, rsr, sg, kp, hst, hsb, hrt, hrb, hrelay, w, v,
+    v_sem, pre_rs_s, pre_rs_r, pre_ag_s, pre_ag_r, ld_sem, kp_sem, z_s, z_r, ref_s, ref_r, rs_s, rs_r, ag_s, ag_r, h_s, h_r, part_s, part_r, relay_s,
     *, n_state, scale, n_members,
 ):
     f32 = jnp.float32
@@ -29,6 +29,19 @@
     zpeer = (1 - tm, mb, st)
     up, down = (tm, mb, st - 1), (tm, mb, st + 1)
     has_up, has_down = st > 0, st < n_state - 1
+    cut = n_state // 2
+    parts = half // 2
+    over, under = st == cut - 1, st == cut
+    at_cut = jnp.logical_or(over, under)
+    hop = jnp.where(st < cut, cut - 1 - st, st - cut)
+    is_relay = jnp.logical_and(lax.rem(hop, 2) == 0, jnp.logical_and(hop > 0, hop < 2 * parts - 2))
+    turn_of = hop // 2
+
+    def lower(p):
+        return (tm, mb, cut + 2 * p)
+
+    def upper(p):
+        return (tm, mb, cut - 1 - 2 * p)
 
     def turn(i):
         return lax.rem(mb + i, 4)
@@ -66,6 +79,17 @@
     for i in (1, 2, 3):
         pl.semaphore_signal(barrier, inc=1, device_id=ypeer(i), device_id_type=MESH)
 
+    @pl.when(at_cut)
+    def _():
+        for p in range(1, parts - 1):
+            pl.semaphore_signal(barrier, inc=1, device_id=lower(p), device_id_type=MESH)
+            pl.semaphore_signal(barrier, inc=1, device_id=upper(p), device_id_type=MESH)
+
+    @pl.when(is_relay)
+    def _():
+        pl.semaphore_signal(barrier, inc=1, device_id=lower(0), device_id_type=MESH)
+        pl.semaphore_signal(barrier, inc=1, device_id=upper(0), device_id_type=MESH)
+
     @pl.when(has_up)
     def _():
         pl.semaphore_signal(barrier, inc=1, device_id=up, device_id_type=MESH)
@@ -139,6 +163,58 @@
 
     def f_down():
         return remote(hsb, hrt, h_s.at[3], h_r.at[3], down)
+
+    def f_up_part(p):
+        lv = pl.ds(2 * p, 2)
+        if p == 0:
+            return remote(hst.at[lv], hrb.at[lv], h_s.at[2], h_r.at[2], up)
+        if p == parts - 1:
+            return remote(hst.at[lv], hrb.at[lv], part_s.at[p - 1], part_r.at[p - 1], up)
+        return remote(hst.at[lv], hrelay, part_s.at[p - 1], part_r.at[3], upper(p))
+
+    def f_down_part(p):
+        lv = pl.ds(2 * p, 2)
+        if p == 0:
+            return remote(hsb.at[lv], hrt.at[lv], h_s.at[3], h_r.at[3], down)
+        if p == parts - 1:
+            return remote(hsb.at[lv], hrt.at[lv], part_s.at[p - 1], part_r.at[p - 1], down)
+        return remote(hsb.at[lv], hrelay, part_s.at[p - 1], part_r.at[3], lower(p))
+
+    def relay_up():
+        dst = hrb.at[pl.ds(2 * turn_of, 2)]
+        return remote(hrelay, dst, relay_s, part_r.at[turn_of - 1], upper(0))
+
+    def relay_down():
+        dst = hrt.at[pl.ds(2 * turn_of, 2)]
+        return remote(hrelay, dst, relay_s, part_r.at[turn_of - 1], lower(0))
+
+    def part_arrival(dst, p):
+        here = dst.at[pl.ds(2 * p, 2)]
+        return remote(here, here, part_s.at[p - 1], part_r.at[p - 1], zpeer)
+
+    def pass_on():
+        @pl.when(is_relay)
+        def _():
+            remote(hrelay, hrelay, relay_s, part_r.at[3], zpeer).wait_recv()
+
+            @pl.when(st < cut)
+            def _():
+                relay_up().start()
+
+            @pl.when(st > cut)
+            def _():
+                relay_down().start()
+
+    def parts_arrive():
+        @pl.when(over)
+        def _():
+            for p in range(1, parts):
+                part_arrival(hrb, p).wait_recv()
+
+        @pl.when(under)
+        def _():
+            for p in range(1, parts):
+                part_arrival(hrt, p).wait_recv()
 
     def products(s, i):
         j, q = 4 * s + i, turn(i)
@@ -185,6 +261,7 @@
         if isinstance(i, int) and i == 0:
             if s == 0:
                 peers = 4 + has_up.astype(jnp.int32) + has_down.astype(jnp.int32)
+                peers = peers + 2 * (parts - 2) * at_cut.astype(jnp.int32) + 2 * is_relay.astype(jnp.int32)
                 pl.semaphore_wait(barrier, peers)
             for n in (1, 2, 3):
                 ref_copy(s, n).start()
@@ -363,7 +440,15 @@
         @pl.when(has_up)
         def _():
             lax.fori_loop(0, half, body, 0)
-            f_up().start()
+
+            @pl.when(under)
+            def _():
+                for p in range(parts):
+                    f_up_part(p).start()
+
+            @pl.when(jnp.logical_not(under))
+            def _():
+                f_up().start()
 
     def edge_bottom():
         def body(l, c):
@@ -374,7 +459,15 @@
         @pl.when(has_down)
         def _():
             lax.fori_loop(0, half, body, 0)
-            f_down().start()
+
+            @pl.when(over)
+            def _():
+                for p in range(parts):
+                    f_down_part(p).start()
+
+            @pl.when(jnp.logical_not(over))
+            def _():
+                f_down().start()
 
     def smooth(l, ks=(0, 1)):
         for k in ks:
@@ -407,12 +500,26 @@
         @pl.when(has_up)
         def _():
             k_down().wait_recv()
-            f_down().wait_recv()
+
+            @pl.when(under)
+            def _():
+                f_down_part(0).wait_recv()
+
+            @pl.when(jnp.logical_not(under))
+            def _():
+                f_down().wait_recv()
 
         @pl.when(has_down)
         def _():
             k_up().wait_recv()
-            f_up().wait_recv()
+
+            @pl.when(over)
+            def _():
+                f_up_part(0).wait_recv()
+
+            @pl.when(jnp.logical_not(over))
+            def _():
+                f_up().wait_recv()
 
     w[pl.ds(0, 8)] = jnp.zeros((8, w.shape[1]), f32)
     w[pl.ds(56, 8)] = jnp.zeros((8, w.shape[1]), f32)
@@ -420,6 +527,54 @@
     zr[mb, pl.ds(post, 2), 1, pl.ds(40, 8)] = jnp.zeros((2, 8, quarter), f32)
     v[pl.ds(0, 8)] = jnp.zeros((8, v.shape[1]), f32)
     v[pl.ds(72, 8)] = jnp.zeros((8, v.shape[1]), f32)
+
+    def mid_sent(l):
+        for i in range(4):
+            z_mid(l, i).wait_send()
+
+    def sums_sent(u):
+        for i in (1, 2, 3):
+            rs_copy(u, i).wait_send()
+            ag_copy(u, i).wait_send()
+
+    def edges_sent():
+        @pl.when(is_relay)
+        def _():
+            remote(hrelay, hrelay, relay_s, part_r.at[3], zpeer).wait_send()
+
+        for u in range(2):
+            for i in range(4):
+                z_edge(u, i).wait_send()
+            sums_sent(u)
+        for i in (1, 2, 3):
+            ref_copy(0, i).wait_send()
+            ref_copy(2, i).wait_send()
+
+        @pl.when(has_up)
+        def _():
+            k_up().wait_send()
+
+            @pl.when(under)
+            def _():
+                for p in range(parts):
+                    f_up_part(p).wait_send()
+
+            @pl.when(jnp.logical_not(under))
+            def _():
+                f_up().wait_send()
+
+        @pl.when(has_down)
+        def _():
+            k_down().wait_send()
+
+            @pl.when(over)
+            def _():
+                for p in range(parts):
+                    f_down_part(p).wait_send()
+
+            @pl.when(jnp.logical_not(over))
+            def _():
+                f_down().wait_send()
 
     def start_mid(l):
         for i in range(4):
@@ -447,6 +602,7 @@
     edge_bottom()
     arrive_mid(1)
     total(2)
+    pass_on()
     pre_total()
     arrive_mid(2)
     total(3)
@@ -456,12 +612,16 @@
     pre_centred()
     for n in range(4):
         z_last(n).start()
+    edges_sent()
+    parts_arrive()
 
     def rest(l, c):
         arrive_mid(l)
         total(l + 1)
         centred(l)
         smooth(l - 2)
+        mid_sent(l - 3)
+        sums_sent(l - 1)
         return c
 
     lax.fori_loop(3, post, rest, 0)
@@ -472,50 +632,23 @@
     smooth(post, (0,))
     centred(post + 1)
     smooth(post - 1)
+    for n in (post - 3, post - 2, post - 1):
+        mid_sent(n)
+        sums_sent(n + 2)
     arrive_last(1)
     smooth(post, (1,))
-    for k in range(2):
-        arrive_last(2 + k)
-        smooth(post + 1, (k,))
-
-    for u in range(2):
-        for i in range(4):
-            z_edge(u, i).wait_send()
-    for n in range(4):
-        z_last(n).wait_send()
-
-    def sent(l, c):
-        for i in range(4):
-            z_mid(l, i).wait_send()
-        return c
-
-    lax.fori_loop(0, post, sent, 0)
+    arrive_last(2)
+    smooth(post + 1, (0,))
     for i in (1, 2, 3):
         pre_rs(i).wait_send()
         pre_ag(i).wait_send()
-        for s in (0, 2):
-            ref_copy(s, i).wait_send()
-        for u in (0, 1):
-            rs_copy(u, i).wait_send()
-            ag_copy(u, i).wait_send()
-
-    def sums_sent(u, c):
-        for i in (1, 2, 3):
-            rs_copy(u, i).wait_send()
-            ag_copy(u, i).wait_send()
-        return c
-
-    lax.fori_loop(2, post + 2, sums_sent, 0)
-
-    @pl.when(has_up)
-    def _():
-        k_up().wait_send()
-        f_up().wait_send()
-
-    @pl.when(has_down)
-    def _():
-        k_down().wait_send()
-        f_down().wait_send()
+    z_last(0).wait_send()
+    z_last(1).wait_send()
+    arrive_last(3)
+    smooth(post + 1, (1,))
+
+    z_last(2).wait_send()
+    z_last(3).wait_send()
 
 
 def body(members, slot_grad, diffusivity, vertical, *, sizes):
@@ -545,6 +678,7 @@
         pltpu.VMEM((half, 8, lon), f32),
         pltpu.VMEM((half, 8, lon), f32),
         pltpu.VMEM((half, 8, lon), f32),
+        pltpu.VMEM((2, 8, lon), f32),
         pltpu.VMEM((64, lon), f32),
         pltpu.VMEM((80, lon), f32),
         dma,
@@ -564,6 +698,9 @@
         dma((half, 3)),
         dma((4,)),
         dma((4,)),
+        dma((3,)),
+        dma((4,)),
+        dma,
     ]
     hbm = pl.BlockSpec(memory_space=pltpu.HBM)
     return pl.pallas_call(

time: 111 us -> 109 us (0.982)
  Pallas kernels: 108 us -> 106 us
    pallas_call x1, Pallas kernels: 108 us -> 106 us  [body(): pl.pallas_call(functools.partial(kernel, n_state=sizes['state'], scale=fl...]
where the time goes in v3:
time: 109 us; the launch traced here: 108 us
  Pallas kernels  106 us (97%)
  local copies, waits for them, and re-layouts  2.19 us (2%)
    pallas_call x1, Pallas kernels, body(): pl.pallas_call(functools.partial(kernel, n_state=sizes['state'], scale=fl...  106 us
    unnamed x1, local copies, waits for them, and re-layouts  2.19 us

profile of v3, /device:TPU:38, one launch (start us, length us, event | category | flops | bytes accessed | tf_op | source)
XLA Modules:
  0.0 108.0 jit_solution(16436336452685943592)
XLA Ops:
  0.0 105.8 %shard_map.46 = f32[8,2,48,1536]{3,2,1,0:T(8,128)S(1)} custom-call(bf16[2,2,16,48,1536]{4,3,2,1,0:T(8,128)(2,1)} %members.1, f32[2,16,48,1536]{3,2,1,0:T(8,128)} %slot_grad.1, f32[48,1536]{1,0:T(8,128)} %diffusivity.1, f32[16,16]{1,0:T(8,128)} %matrix.1), custom_call_target="tpu_custom_call" | custom-call | tf_op jit(solution)/shard_map/pallas_call | solution.py:706
  105.8 2.2 %copy.6 = f32[8,2,48,1536]{3,2,1,0:T(8,128)} copy(f32[8,2,48,1536]{3,2,1,0:T(8,128)S(1)} %shard_map.46) | data formatting | bytes 9437184

commit v4 on v3

--- a/solution.py
+++ b/solution.py
@@ -109,14 +109,32 @@
         return remote(cs.at[q, :, ks, rows], zr.at[q, :, ks, rows], z_s.at[n], z_r.at[n], zpeer)
 
     def z_mid(l, i):
-        q, n = turn(i), 8 + 4 * l + i
+        q, n = turn(i), 8 + l
         ks = pl.ds(0, 1) if i == 0 else pl.ds(0, 2)
         return remote(cs.at[q, l, ks, mid], zr.at[q, l, ks, mid], z_s.at[n], z_r.at[n], zpeer)
 
     def z_last(n):
-        at = 8 + 4 * post + n
+        at = 8 + post + n
         l, k = post + n // 2, n % 2
         return remote(cs.at[:, l, k, mid], zr.at[:, l, k, mid], z_s.at[at], z_r.at[at], zpeer)
+
+    def z_mid_all(l):
+        size = rb.at[0, pl.ds(0, 7), mid]
+        return remote(size, size, z_s.at[8 + l], z_r.at[8 + l], zpeer)
+
+    def three(u, send, recv):
+        lv, rows = span(u)
+        size = rsr.at[:, lv, rows]
+        return remote(size, size, send.at[u], recv.at[u], zpeer)
+
+    def rs_all(u):
+        return three(u, rs_s, rs_r)
+
+    def ag_all(u):
+        return three(u, ag_s, ag_r)
+
+    def pre_all(send, recv):
+        return remote(pr, pr, send, recv, zpeer)
 
     ref_part = ((pl.ds(0, post), pl.ds(8, 8)), (pl.ds(0, half), pl.ds(32, 16)), (pl.ds(0, post), pl.ds(16, 16)))
 
@@ -139,18 +157,18 @@
     def rs_copy(u, i):
         lv, rows = span(u)
         q = turn(i)
-        return remote(ps.at[q, lv, rows], rsr.at[i - 1, lv, rows], rs_s.at[u, i - 1], rs_r.at[u, i - 1], ypeer(i))
+        return remote(ps.at[q, lv, rows], rsr.at[i - 1, lv, rows], rs_s.at[u], rs_r.at[u], ypeer(i))
 
     def ag_copy(u, i):
         lv, rows = span(u)
         here = sg.at[mb, lv, rows]
-        return remote(here, here, ag_s.at[u, i - 1], ag_r.at[u, i - 1], ypeer(i))
+        return remote(here, here, ag_s.at[u], ag_r.at[u], ypeer(i))
 
     def pre_rs(i):
-        return remote(pp.at[turn(i)], pr.at[i - 1], pre_rs_s.at[i - 1], pre_rs_r.at[i - 1], ypeer(i))
+        return remote(pp.at[turn(i)], pr.at[i - 1], pre_rs_s, pre_rs_r, ypeer(i))
 
     def pre_ag(i):
-        return remote(pg.at[mb], pg.at[mb], pre_ag_s.at[i - 1], pre_ag_r.at[i - 1], ypeer(i))
+        return remote(pg.at[mb], pg.at[mb], pre_ag_s, pre_ag_r, ypeer(i))
 
     def k_up():
         return remote(kp.at[pl.ds(8, 8)], kp.at[pl.ds(56, 8)], h_s.at[0], h_r.at[0], up)
@@ -345,16 +363,15 @@
             rs_copy(u, i).start()
 
     def arrive_mid(l):
+        z_mid_all(l).wait_recv()
         for i in range(4):
-            z_mid(l, i).wait_recv()
             add_up(turn(i), l, mid)
             if i:
                 rs_copy(2 + l, i).start()
 
     def total(u):
         lv, rows = span(u)
-        for i in (1, 2, 3):
-            rs_copy(u, i).wait_recv()
+        rs_all(u).wait_recv()
 
         def body(l, c):
             sg[mb, l, rows] = (ps[mb, l, rows] + rsr[0, l, rows]) + (rsr[1, l, rows] + rsr[2, l, rows])
@@ -366,13 +383,7 @@
 
     def centred(u):
         lv, rows = span(u)
-        for i in (1, 2, 3):
-            q = turn(i)
-            pltpu.make_async_remote_copy(
-                src_ref=sg.at[q, lv, rows], dst_ref=sg.at[q, lv, rows],
-                send_sem=ag_s.at[u, 3 - i], recv_sem=ag_r.at[u, 3 - i],
-                device_id=zpeer, device_id_type=MESH,
-            ).wait_recv()
+        ag_all(u).wait_recv()
 
         def body(l, c):
             for q in range(4):
@@ -397,8 +408,7 @@
                 pre_rs(n).start()
 
     def pre_total():
-        for i in (1, 2, 3):
-            pre_rs(i).wait_recv()
+        pre_all(pre_rs_s, pre_rs_r).wait_recv()
 
         def add(l, c):
             for h in range(2):
@@ -410,9 +420,8 @@
             pre_ag(i).start()
 
     def pre_centred():
+        pre_all(pre_ag_s, pre_ag_r).wait_recv()
         for i in (1, 2, 3):
-            here = pg.at[turn(i)]
-            remote(here, here, pre_ag_s.at[3 - i], pre_ag_r.at[3 - i], zpeer).wait_recv()
             ref_copy(1, i).wait_send()
 
         def centre(q, c):
@@ -529,13 +538,11 @@
     v[pl.ds(72, 8)] = jnp.zeros((8, v.shape[1]), f32)
 
     def mid_sent(l):
-        for i in range(4):
-            z_mid(l, i).wait_send()
+        z_mid_all(l).wait_send()
 
     def sums_sent(u):
-        for i in (1, 2, 3):
-            rs_copy(u, i).wait_send()
-            ag_copy(u, i).wait_send()
+        rs_all(u).wait_send()
+        ag_all(u).wait_send()
 
     def edges_sent():
         @pl.when(is_relay)
@@ -639,9 +646,8 @@
     smooth(post, (1,))
     arrive_last(2)
     smooth(post + 1, (0,))
-    for i in (1, 2, 3):
-        pre_rs(i).wait_send()
-        pre_ag(i).wait_send()
+    pre_all(pre_rs_s, pre_rs_r).wait_send()
+    pre_all(pre_ag_s, pre_ag_r).wait_send()
     z_last(0).wait_send()
     z_last(1).wait_send()
     arrive_last(3)
@@ -682,20 +688,20 @@
         pltpu.VMEM((64, lon), f32),
         pltpu.VMEM((80, lon), f32),
         dma,
-        dma((3,)),
-        dma((3,)),
-        dma((3,)),
-        dma((3,)),
+        dma,
+        dma,
+        dma,
+        dma,
         dma((12, 2)),
         dma,
-        dma((12 + 4 * (half - 2),)),
-        dma((12 + 4 * (half - 2),)),
+        dma((10 + half,)),
+        dma((10 + half,)),
         dma((3, 3)),
         dma((3, 3)),
-        dma((half, 3)),
-        dma((half, 3)),
-        dma((half, 3)),
-        dma((half, 3)),
+        dma((half,)),
+        dma((half,)),
+        dma((half,)),
+        dma((half,)),
         dma((4,)),
         dma((4,)),
         dma((3,)),

time: 109 us -> 108 us (level)
  no operation moved by 1% of the time
where the time goes in v4:
time: 108 us; the launch traced here: 107 us
  Pallas kernels  105 us (97%)
  local copies, waits for them, and re-layouts  2.19 us (2%)
    pallas_call x1, Pallas kernels, body(): pl.pallas_call(functools.partial(kernel, n_state=sizes['state'], scale=fl...  105 us
    unnamed x1, local copies, waits for them, and re-layouts  2.19 us

profile of v4, /device:TPU:38, one launch (start us, length us, event | category | flops | bytes accessed | tf_op | source)
XLA Modules:
  0.0 107.1 jit_solution(2444418597907919653)
XLA Ops:
  0.0 104.9 %shard_map.46 = f32[8,2,48,1536]{3,2,1,0:T(8,128)S(1)} custom-call(bf16[2,2,16,48,1536]{4,3,2,1,0:T(8,128)(2,1)} %members.1, f32[2,16,48,1536]{3,2,1,0:T(8,128)} %slot_grad.1, f32[48,1536]{1,0:T(8,128)} %diffusivity.1, f32[16,16]{1,0:T(8,128)} %matrix.1), custom_call_target="tpu_custom_call" | custom-call | tf_op jit(solution)/shard_map/pallas_call | solution.py:712
  104.9 2.2 %copy.6 = f32[8,2,48,1536]{3,2,1,0:T(8,128)} copy(f32[8,2,48,1536]{3,2,1,0:T(8,128)S(1)} %shard_map.46) | data formatting | bytes 9437184

commit v5 on v4

--- a/solution.py
+++ b/solution.py
@@ -30,11 +30,11 @@
     up, down = (tm, mb, st - 1), (tm, mb, st + 1)
     has_up, has_down = st > 0, st < n_state - 1
     cut = n_state // 2
-    parts = half // 2
+    parts, share = 3, hrelay.shape[0]
     over, under = st == cut - 1, st == cut
     at_cut = jnp.logical_or(over, under)
     hop = jnp.where(st < cut, cut - 1 - st, st - cut)
-    is_relay = jnp.logical_and(lax.rem(hop, 2) == 0, jnp.logical_and(hop > 0, hop < 2 * parts - 2))
+    is_relay = jnp.logical_and(lax.rem(hop, 2) == 0, jnp.logical_and(hop > 0, hop < 2 * parts))
     turn_of = hop // 2
 
     def lower(p):
@@ -60,9 +60,14 @@
         rows = pl.ds(block_rows[s], 16)
         lanes = pl.ds(pl.multiple_of(turn(i) * quarter, LANES), quarter)
         j = 4 * s + i
+        if isinstance(i, int) and i == 0:
+            place = (0, 1, 8)[s]
+        else:
+            place = (i + 1, i + 4, i + 8)[s]
+        slot = lax.rem(place, 4)
         return (
-            pltpu.make_async_copy(members.at[:, :, :, rows, lanes], mv.at[j], ld_sem.at[j, 0]),
-            pltpu.make_async_copy(slot_grad.at[:, :, rows, lanes], gv.at[j], ld_sem.at[j, 1]),
+            pltpu.make_async_copy(members.at[:, :, :, rows, lanes], mv.at[j], ld_sem.at[slot, 0]),
+            pltpu.make_async_copy(slot_grad.at[:, :, rows, lanes], gv.at[j], ld_sem.at[slot, 1]),
         )
 
     def start_loads(s, i):
@@ -81,7 +86,7 @@
 
     @pl.when(at_cut)
     def _():
-        for p in range(1, parts - 1):
+        for p in range(1, parts):
             pl.semaphore_signal(barrier, inc=1, device_id=lower(p), device_id_type=MESH)
             pl.semaphore_signal(barrier, inc=1, device_id=upper(p), device_id_type=MESH)
 
@@ -182,32 +187,34 @@
     def f_down():
         return remote(hsb, hrt, h_s.at[3], h_r.at[3], down)
 
+    def part_levels(p):
+        first = half - share * (parts - 1)
+        if isinstance(p, int) and p == 0:
+            return pl.ds(0, first)
+        return pl.ds(first + share * (p - 1), share)
+
     def f_up_part(p):
-        lv = pl.ds(2 * p, 2)
+        lv = part_levels(p)
         if p == 0:
             return remote(hst.at[lv], hrb.at[lv], h_s.at[2], h_r.at[2], up)
-        if p == parts - 1:
-            return remote(hst.at[lv], hrb.at[lv], part_s.at[p - 1], part_r.at[p - 1], up)
         return remote(hst.at[lv], hrelay, part_s.at[p - 1], part_r.at[3], upper(p))
 
     def f_down_part(p):
-        lv = pl.ds(2 * p, 2)
+        lv = part_levels(p)
         if p == 0:
             return remote(hsb.at[lv], hrt.at[lv], h_s.at[3], h_r.at[3], down)
-        if p == parts - 1:
-            return remote(hsb.at[lv], hrt.at[lv], part_s.at[p - 1], part_r.at[p - 1], down)
         return remote(hsb.at[lv], hrelay, part_s.at[p - 1], part_r.at[3], lower(p))
 
     def relay_up():
-        dst = hrb.at[pl.ds(2 * turn_of, 2)]
+        dst = hrb.at[part_levels(turn_of)]
         return remote(hrelay, dst, relay_s, part_r.at[turn_of - 1], upper(0))
 
     def relay_down():
-        dst = hrt.at[pl.ds(2 * turn_of, 2)]
+        dst = hrt.at[part_levels(turn_of)]
         return remote(hrelay, dst, relay_s, part_r.at[turn_of - 1], lower(0))
 
     def part_arrival(dst, p):
-        here = dst.at[pl.ds(2 * p, 2)]
+        here = dst.at[part_levels(p)]
         return remote(here, here, part_s.at[p - 1], part_r.at[p - 1], zpeer)
 
     def pass_on():
@@ -279,12 +286,14 @@
         if isinstance(i, int) and i == 0:
             if s == 0:
                 peers = 4 + has_up.astype(jnp.int32) + has_down.astype(jnp.int32)
-                peers = peers + 2 * (parts - 2) * at_cut.astype(jnp.int32) + 2 * is_relay.astype(jnp.int32)
+                peers = peers + 2 * (parts - 1) * at_cut.astype(jnp.int32) + 2 * is_relay.astype(jnp.int32)
                 pl.semaphore_wait(barrier, peers)
-            for n in (1, 2, 3):
-                ref_copy(s, n).start()
             if s == 0:
                 z_edge(0, i).start()
+            else:
+                for at in (1, 0) if s == 1 else (2,):
+                    for n in (1, 2, 3):
+                        ref_copy(at, n).start()
             subtract(s, mb, lambda l, rows: cs[mb, l, 1, rows], (0,))
         elif s == 0:
             z_edge(0, i).start()
@@ -684,7 +693,7 @@
         pltpu.VMEM((half, 8, lon), f32),
         pltpu.VMEM((half, 8, lon), f32),
         pltpu.VMEM((half, 8, lon), f32),
-        pltpu.VMEM((2, 8, lon), f32),
+        pltpu.VMEM((3, 8, lon), f32),
         pltpu.VMEM((64, lon), f32),
         pltpu.VMEM((80, lon), f32),
         dma,
@@ -692,7 +701,7 @@
         dma,
         dma,
         dma,
-        dma((12, 2)),
+        dma((4, 2)),
         dma,
         dma((10 + half,)),
         dma((10 + half,)),

time: 108 us -> 107 us (level)
    pallas_call x1, Pallas kernels: 105 us -> 104 us  [body(): pl.pallas_call(functools.partial(kernel, n_state=sizes['state'], scale=fl...]
where the time goes in v5:
time: 107 us; the launch traced here: 106 us
  Pallas kernels  104 us (97%)
  local copies, waits for them, and re-layouts  2.19 us (2%)
    pallas_call x1, Pallas kernels, body(): pl.pallas_call(functools.partial(kernel, n_state=sizes['state'], scale=fl...  104 us
    unnamed x1, local copies, waits for them, and re-layouts  2.19 us

profile of v5, /device:TPU:38, one launch (start us, length us, event | category | flops | bytes accessed | tf_op | source)
XLA Modules:
  0.0 105.9 jit_solution(8681863301928649818)
XLA Ops:
  0.0 103.7 %shard_map.46 = f32[8,2,48,1536]{3,2,1,0:T(8,128)S(1)} custom-call(bf16[2,2,16,48,1536]{4,3,2,1,0:T(8,128)(2,1)} %members.1, f32[2,16,48,1536]{3,2,1,0:T(8,128)} %slot_grad.1, f32[48,1536]{1,0:T(8,128)} %diffusivity.1, f32[16,16]{1,0:T(8,128)} %matrix.1), custom_call_target="tpu_custom_call" | custom-call | tf_op jit(solution)/shard_map/pallas_call | solution.py:721
  103.7 2.2 %copy.6 = f32[8,2,48,1536]{3,2,1,0:T(8,128)} copy(f32[8,2,48,1536]{3,2,1,0:T(8,128)S(1)} %shard_map.46) | data formatting | bytes 9437184
